TPU v7x, 128 devices: a whole 4x4x4 slice. The times are simulated.
128 devices in a mesh: kpt: 2 (over x_lo), grid: 64 (over x_hi, z, y, core).
Axes of the slice: x: 4 (x_hi: 2, x_lo: 2; x = x_hi * 2 + x_lo), y: 4, z: 4, core: 2. Of those that a mesh axis runs over, the one named last changes fastest.
Arguments:
- orbitals: bfloat16 [4, 2, 2, 512, 256, 256], P('kpt', None, None, 'grid'), may hold values from -6 to 6
- kweights: int32 [4], P('kpt'), may hold values from 1 to 16
- occupations: int32 [4, 2], P('kpt'), may hold values from 0 to 2
- z_basis: float32 [512, 512], replicated, may hold values from -0.25 to 0.25
- z_eigen: float32 [512], replicated, may hold values from 0.25 to 4
Outputs:
- potential: float32 [512, 256, 256], P('grid')
All inputs are finite; a program needn't handle non-finite values.
Results may differ from a plain program's by a relative error of at most 0.0003.
Values sent between devices are 32-bit elements; how exact they have to be, the bound alone decides.
A program may use at most 64 MiB of HBM per device.

v0:
```python
from functools import partial

import jax
import jax.numpy as jnp
from jax import lax
from jax.sharding import PartitionSpec as P

precise = lax.Precision.HIGHEST


def in_blocks(shard, dim, peers):
    before, after = (shard.shape[:dim], shard.shape[dim + 1 :])
    return jnp.moveaxis(shard.reshape(*before, peers, -1, *after), dim, 0)


def summed_on_arrival(shard, axis, dim):
    parts = in_blocks(shard, dim, lax.axis_size(axis))
    arrived = lax.all_to_all(parts, axis, split_axis=0, concat_axis=0, tiled=True)
    return arrived.sum(axis=0)


def copy_for_each(shard, axis):
    copies = jnp.broadcast_to(shard, (lax.axis_size(axis), *shard.shape))
    return lax.all_to_all(copies, axis, split_axis=0, concat_axis=0, tiled=True)


def laid_out(parts, dim):
    dims = list(parts.shape[1:])
    dims[dim] *= parts.shape[0]
    return jnp.moveaxis(parts, 0, dim).reshape(dims)


def gather_directly(shard, axis, dim):
    parts = copy_for_each(shard, axis)
    return laid_out(parts, dim)


def real_basis(length):
    position = jnp.arange(length, dtype=jnp.int32)
    product = position[:, None] * position[None, :] % length
    angles = product.astype(jnp.float32) * (2.0 * jnp.pi / length)
    lower = position[:, None] <= length // 2
    table = jnp.where(lower, jnp.cos(angles), jnp.sin(angles))
    edges = (position == 0) | (position == length // 2)
    weights = jnp.where(edges, 1.0, 2.0).astype(jnp.float32) / length
    return (table, table * weights[:, None])


def forward_real(density, bases):
    table_x, scaled_x, table_y, scaled_y = bases
    along = jnp.einsum("zxy,ky->zxk", density, table_y, precision=precise)
    return jnp.einsum("jx,zxk->zjk", table_x, along, precision=precise)[None]


def inverse_real(planes, bases):
    table_x, scaled_x, table_y, scaled_y = bases
    half_done = jnp.einsum("jx,zjk->zxk", scaled_x, planes[0], precision=precise)
    return jnp.einsum("zxk,ky->zxy", half_done, scaled_y, precision=precise)


def scale_table(z_eigen, kx_start, kx_count, x_length, y_length):
    wave_x = (kx_start + jnp.arange(kx_count, dtype=jnp.int32)).astype(jnp.float32)
    wave_y = jnp.arange(y_length, dtype=jnp.int32).astype(jnp.float32)
    shift_x = 2.0 * jnp.sin(jnp.pi * wave_x / x_length)
    shift_y = 2.0 * jnp.sin(jnp.pi * wave_y / y_length)
    shifted = shift_x[:, None] ** 2 + shift_y[None, :] ** 2
    return 1.0 / (z_eigen[:, None, None] + shifted[None])


def kernel_columns(z_rows, factors, columns):
    projected = jnp.einsum("zj,czab->cjab", z_rows, columns, precision=precise)
    return jnp.einsum("zj,cjab->czab", z_rows, projected * factors[None], precision=precise)


def on_device(orbitals, kweights, occupations, z_basis, z_eigen):
    points = orbitals.shape[0]
    band_count = orbitals.shape[1]
    x_length = orbitals.shape[4]
    y_length = orbitals.shape[5]
    z_length = z_basis.shape[0]
    factor = (kweights[:, None] * occupations).astype(jnp.float32) / (16.0 * points * band_count)
    values = orbitals.astype(jnp.float32)
    partial_sum = jnp.sum(factor[:, :, None, None, None, None] * values * values, axis=(0, 1, 2))
    table_x, scaled_x = real_basis(x_length)
    table_y, scaled_y = real_basis(y_length)
    forward = partial(forward_real, bases=(table_x, scaled_x, table_y, scaled_y))
    inverse = partial(inverse_real, bases=(table_x, scaled_x, table_y, scaled_y))
    groups = lax.axis_size("kpt")
    blocks = lax.axis_size("grid")
    density = summed_on_arrival(partial_sum, "kpt", 0)
    spectrum = forward(density)
    kx_count = x_length // (groups * blocks)
    kx_start = (lax.axis_index("kpt") * blocks + lax.axis_index("grid")) * kx_count
    z_count = z_length // (groups * blocks)
    z_rows = (
        z_basis.reshape(blocks, groups, z_count, z_length)
        .transpose(1, 0, 2, 3)
        .reshape(z_length, z_length)
    )
    factors = scale_table(z_eigen, kx_start, kx_count, x_length, y_length)
    columns = kernel_columns(
        z_rows,
        factors,
        lax.all_to_all(spectrum, ("kpt", "grid"), split_axis=2, concat_axis=1, tiled=True),
    )
    planes = lax.all_to_all(columns, ("kpt", "grid"), split_axis=1, concat_axis=2, tiled=True)
    potential = gather_directly(inverse(planes), "kpt", 0)
    return potential


def solution(mesh):
    return jax.shard_map(
        on_device,
        mesh=mesh,
        in_specs=(P("kpt", None, None, "grid", None, None), P("kpt"), P("kpt", None), P(), P()),
        out_specs=P("grid", None, None),
        check_vma=False,
    )
```

profile of v0, /device:TPU:1, one launch (start us, length us, event | category | flops | bytes accessed | tf_op | source)
XLA Modules:
  0.0 137.6 jit_solution(10050995222508390342)
XLA Ops:
  0.0 0.8 convert_multiply_fusion
  0.8 7.2 %fusion = f32[8,256,256]{2,1,0:T(8,128)} fusion(bf16[2,2,2,8,256,256]{5,4,3,2,1,0:T(8,128)(2,1)} %param.5, f32[2,2]{1,0:T(2,128)S(1)} %convert_multiply_fusion), kind=kLoop, calls=%fused_computation.1 | loop fusion | flops 16252928 | bytes 10485776 | tf_op jit(solution)/shard_map/reduce_sum | solution.py:83
  8.0 3.8 %all-to-all-start = ((f32[2,4,256,256]{3,2,1,0:T(8,128)}), f32[2,4,256,256]{3,2,1,0:T(8,128)S(1)}, u32[]{:S(2)}, u32[]{:S(2)}) async-start(f32[2,4,256,256]{3,2,1,0:T(8,128)} %bitcast.48), calls=%async_computation | async-start | bytes 4194304 | tf_op jit(solution)/shard_map/all_to_all | solution.py:18
  11.8 24.7 %all-to-all-done = f32[2,4,256,256]{3,2,1,0:T(8,128)S(1)} async-done(((f32[2,4,256,256]{3,2,1,0:T(8,128)}), f32[2,4,256,256]{3,2,1,0:T(8,128)S(1)}, u32[]{:S(2)}, u32[]{:S(2)}) %all-to-all-start) | async-done | bytes 2097184 | tf_op jit(solution)/shard_map/all_to_all | solution.py:18
  36.4 0.2 reduce_sum.19
  36.7 0.0 copy-start
  36.7 2.2 %fusion.12 = f32[4,256,256]{1,2,0:T(8,128)S(1)} fusion(f32[4,256,256]{2,1,0:T(8,128)S(1)} %reduce_sum.19, pred[256]{0:T(512)(128)(4,1)S(1)} %iota_compare_fusion), kind=kOutput, calls=%fused_computation.20 | convolution fusion | flops 806289408 | bytes 2097408 | tf_op jit(solution)/shard_map/zxy,ky->zxk/dot_general | solution.py:51
  38.8 2.0 %convolution_bitcast_fusion.3 = f32[1,4,256,256]{2,3,1,0:T(8,128)S(1)} fusion(f32[4,256,256]{1,2,0:T(8,128)S(1)} %fusion.12, pred[256]{0:T(512)(128)(4,1)S(1)} %iota_compare_fusion), kind=kOutput, calls=%fused_computation.7 | convolution fusion | flops 806289408 | bytes 2097408 | tf_op jit(solution)/shard_map/jx,zxk->zjk/dot_general | solution.py:52
  40.9 1.3 copy.24
  42.2 11.9 %all-to-all-start.1 = ((f32[1,4,256,256]{3,1,0,2:T(4,128)}), f32[1,4,256,256]{3,1,0,2:T(4,128)S(1)}, u32[]{:S(2)}, u32[]{:S(2)}) async-start(f32[1,4,256,256]{3,1,0,2:T(4,128)} %copy.24), calls=%async_computation.1 | async-start | bytes 2097152 | tf_op jit(solution)/shard_map/all_to_all | solution.py:104
  54.1 1.5 %reshape.93 = f32[64,2,4,512]{3,2,1,0:T(4,128)S(1)} reshape(f32[512,512]{1,0:T(8,128)} %param.8) | data formatting | bytes 2097152 | tf_op jit(solution)/shard_map/reshape | solution.py:96
  55.7 0.1 copy.26
  55.7 0.4 reshape.98
  56.2 0.1 broadcast_add_fusion
  56.3 17.4 %all-to-all-done.1 = f32[1,4,256,256]{3,1,0,2:T(4,128)S(1)} async-done(((f32[1,4,256,256]{3,1,0,2:T(4,128)}), f32[1,4,256,256]{3,1,0,2:T(4,128)S(1)}, u32[]{:S(2)}, u32[]{:S(2)}) %all-to-all-start.1) | async-done | bytes 1048608 | tf_op jit(solution)/shard_map/all_to_all | solution.py:104
  73.7 0.5 copy.25
  74.2 0.0 copy-done
  74.2 1.9 %fusion.2 = f32[512,2,256]{0,2,1:T(8,128)S(1)} fusion(f32[512,512,1]{1,0,2:T(8,128)S(1)} %reshape.98, f32[512,2,256]{2,1,0:T(2,128)S(1)} %bitcast.53, f32[2,256]{1,0:T(2,128)S(1)} %broadcast_add_fusion, f32[512]{0:T(512)S(1)} %copy-done), kind=kOutput, calls=%fused_computation.6 | convolution fusion | flops 1611399168 | bytes 3149824 | tf_op jit(solution)/shard_map/zj,czab->cjab/dot_general | solution.py:71
  76.2 1.9 %convolution_bitcast_fusion.1 = f32[1,512,2,256]{1,3,2,0:T(8,128)S(1)} fusion(f32[512,2,256]{0,2,1:T(8,128)S(1)} %fusion.2, f32[512,512,1]{1,0,2:T(8,128)S(1)} %reshape.98), kind=kOutput, calls=%fused_computation.3 | convolution fusion | flops 1610612736 | bytes 3145728 | tf_op jit(solution)/shard_map/zj,cjab->czab/dot_general | solution.py:72
  78.0 1.3 copy.28
  79.3 4.2 %all-to-all-start.2 = ((f32[1,512,2,256]{3,2,0,1:T(2,128)}), f32[1,512,2,256]{3,2,0,1:T(2,128)S(1)}, u32[]{:S(2)}, u32[]{:S(2)}) async-start(f32[1,512,2,256]{3,2,0,1:T(2,128)} %copy.28), calls=%async_computation.2 | async-start | bytes 2097152 | tf_op jit(solution)/shard_map/all_to_all | solution.py:106
  83.6 19.6 %all-to-all-done.2 = f32[1,512,2,256]{3,2,0,1:T(2,128)S(1)} async-done(((f32[1,512,2,256]{3,2,0,1:T(2,128)}), f32[1,512,2,256]{3,2,0,1:T(2,128)S(1)}, u32[]{:S(2)}, u32[]{:S(2)}) %all-to-all-start.2) | async-done | bytes 1048608 | tf_op jit(solution)/shard_map/all_to_all | solution.py:106
  103.1 0.3 copy.29
  103.4 2.8 %convolution_bitcast_fusion = f32[4,256,256]{1,2,0:T(8,128)S(1)} fusion(f32[4,256,256]{2,0,1:T(4,128)S(1)} %bitcast.51, f32[256]{0:T(256)S(1)} %fusion.21, pred[256]{0:T(512)(128)(4,1)S(1)} %iota_compare_fusion), kind=kOutput, calls=%fused_computation.2 | convolution fusion | flops 806354944 | bytes 2098432 | tf_op jit(solution)/shard_map/jx,zjk->zxk/dot_general | solution.py:57
  106.2 2.8 %fusion.8 = f32[4,256,256]{2,1,0:T(8,128)S(1)} fusion(f32[4,256,256]{1,2,0:T(8,128)S(1)} %convolution_bitcast_fusion, f32[256]{0:T(256)S(1)} %fusion.21, pred[256]{0:T(512)(128)(4,1)S(1)} %iota_compare_fusion), kind=kOutput, calls=%fused_computation.16 | convolution fusion | flops 806354944 | bytes 2098432 | tf_op jit(solution)/shard_map/zxk,ky->zxy/dot_general | solution.py:58
  109.0 0.2 broadcast_in_dim.49
  109.2 27.0 %all_to_all.40 = f32[2,4,256,256]{3,2,1,0:T(8,128)S(1)} all-to-all(f32[2,4,256,256]{3,2,1,0:T(8,128)S(1)} %broadcast_in_dim.49), channel_id=1, replica_groups=mesh['kpt'=2,'grid'=64] {'kpt'}, dimensions={0} | all-to-all | bytes 4194304 | tf_op jit(solution)/shard_map/all_to_all | solution.py:24
  136.3 1.3 copy.39
  (4 shorter events, 0.1 us)
Async XLA Ops:
  8.0 28.4 %all-to-all-start = ((f32[2,4,256,256]{3,2,1,0:T(8,128)}), f32[2,4,256,256]{3,2,1,0:T(8,128)S(1)}, u32[]{:S(2)}, u32[]{:S(2)}) async-start(f32[2,4,256,256]{3,2,1,0:T(8,128)} %bitcast.48), calls=%async_computation | async-start | bytes 4194304 | tf_op jit(solution)/shard_map/all_to_all | solution.py:18
  36.7 37.6 %copy-start = (f32[512]{0:T(512)S(1)}, f32[512]{0:T(512)}, u32[]{:S(2)}) copy-start(f32[512]{0:T(512)} %param.9) | copy-start | bytes 6148
  42.2 31.5 %all-to-all-start.1 = ((f32[1,4,256,256]{3,1,0,2:T(4,128)}), f32[1,4,256,256]{3,1,0,2:T(4,128)S(1)}, u32[]{:S(2)}, u32[]{:S(2)}) async-start(f32[1,4,256,256]{3,1,0,2:T(4,128)} %copy.24), calls=%async_computation.1 | async-start | bytes 2097152 | tf_op jit(solution)/shard_map/all_to_all | solution.py:104
  79.3 23.8 %all-to-all-start.2 = ((f32[1,512,2,256]{3,2,0,1:T(2,128)}), f32[1,512,2,256]{3,2,0,1:T(2,128)S(1)}, u32[]{:S(2)}, u32[]{:S(2)}) async-start(f32[1,512,2,256]{3,2,0,1:T(2,128)} %copy.28), calls=%async_computation.2 | async-start | bytes 2097152 | tf_op jit(solution)/shard_map/all_to_all | solution.py:106
where the time goes:
time: 138 us
  waiting for transfers between devices  61.6 us (45%)
  blocking collectives  27 us (20%)
  starting transfers between devices  19.9 us (14%)
  matrix products  13.6 us (10%)
  other arithmetic  8.38 us (6%)
  local copies, waits for them, and re-layouts  6.89 us (5%)
    all_to_all x1, blocking collectives, copy_for_each(): return lax.all_to_all(copies, axis, split_axis=0, concat_axis=0, tiled=True)  27 us
    all_to_all x1, waiting for transfers between devices, summed_on_arrival(): lax.all_to_all(parts, axis, split_axis=0, concat_axis=0, tiled=True)  24.7 us
    all_to_all x1, waiting for transfers between devices, on_device(): lax.all_to_all(columns, ('kpt', 'grid'), split_axis=1, concat_axis=2, til...  19.6 us
    all_to_all x1, waiting for transfers between devices, on_device(): lax.all_to_all(spectrum, ('kpt', 'grid'), split_axis=2, concat_axis=1, ti...  17.4 us
    all_to_all x1, starting transfers between devices, on_device(): lax.all_to_all(spectrum, ('kpt', 'grid'), split_axis=2, concat_axis=1, ti...  11.9 us
    reduce_sum x1, other arithmetic, on_device(): jnp.sum(factor[:, :, None, None, None, None] * values * values, axis=(0,...  7.22 us
    all_to_all x1, starting transfers between devices, on_device(): lax.all_to_all(columns, ('kpt', 'grid'), split_axis=1, concat_axis=2, til...  4.21 us
    all_to_all x1, starting transfers between devices, summed_on_arrival(): lax.all_to_all(parts, axis, split_axis=0, concat_axis=0, tiled=True)  3.76 us
  transfers between devices with their start and end apart: 3, of which 3 were waited for; matrix products, arithmetic and copies ran while one was open for 2% of the time, Pallas kernels for 0%

commit v1 on v0

v1 whole, which is shorter than its diff:
```python
import functools

import jax
import jax.numpy as jnp
import numpy as np
from jax import lax
from jax.experimental import pallas as pl
from jax.experimental.pallas import tpu as pltpu
from jax.sharding import PartitionSpec as P

MESH = pl.DeviceIdType.MESH
f32 = jnp.float32
bf16 = jnp.bfloat16
N = 256
NZ = 512
LANES = 128
DEVICES = 128
PLANES = 8
QUAD = 4


def real_table():
    position = np.arange(N)
    angles = (position[:, None] * position[None, :] % N) * (2.0 * np.pi / N)
    return np.where(position[:, None] <= N // 2, np.cos(angles), np.sin(angles))


def tables():
    table = real_table()
    halves = []
    for one in (table.T, table):
        high = one.astype(bf16)
        low = (one - high.astype(np.float64)).astype(bf16)
        halves += [high, low]
    return np.stack(halves)


def mode_rows():
    position = np.arange(N)
    shift = (2.0 * np.sin(np.pi * position / N)) ** 2
    edges = (position == 0) | (position == N // 2)
    weight = np.where(edges, 1.0, 2.0) / N
    rows = np.zeros((8, N), np.float32)
    rows[0], rows[1] = shift, weight
    return rows


def split(value):
    high = value.astype(bf16)
    low = (value - high.astype(f32)).astype(bf16)
    return high, low


def dot(left, right):
    return jnp.dot(left, right, preferred_element_type=f32)


def dot3(left_high, left_low, right_high, right_low):
    return dot(left_high, right_high) + (dot(left_high, right_low) + dot(left_low, right_high))


def coords():
    k = lax.axis_index("kpt")
    g = lax.axis_index("grid")
    return g // 32 * 2 + k, lax.rem(g // 2, 4), lax.rem(g // 8, 4), lax.rem(g, 2)


def device(x, y, z, c):
    return lax.rem(x, 2), ((x // 2 * 4 + z) * 4 + y) * 2 + c


def peer(step):
    x, y, z, c = coords()
    mixed = lax.rem(step * 37, 128)
    return device(
        lax.rem(x + lax.rem(mixed, 4), 4),
        lax.rem(y + lax.rem(mixed // 4, 4), 4),
        lax.rem(z + lax.rem(mixed // 16, 4), 4),
        lax.rem(c + mixed // 64, 2),
    )


def rows_of(index, count):
    return pl.ds(pl.multiple_of(index * count, count), count)


def kernel(
    orb, kw, occ, zb, lam, tab_in, row_in, out,
    obuf, zbuf, lamv, tab, rowv, B, R, W, Q, Zh, Zl, ZhT, ZlT, fac,
    dh, dl, Xh, Xl, Yh, Yl, half,
    orb_sem, in_sem, send_sem, recv_sem, back_sem, got_sem, y_sem, z_sem, c_sem,
):
    k = lax.axis_index("kpt")
    g = lax.axis_index("grid")
    me = k * 64 + g
    x, y, z, c = coords()

    def along(axis, step):
        return device(
            lax.rem(x + step, 4) if axis == 0 else x,
            lax.rem(y + step, 4) if axis == 1 else y,
            lax.rem(z + step, 4) if axis == 2 else z,
            lax.rem(c + step, 2) if axis == 3 else c,
        )

    def signal(sem, axis):
        for step in range(1, 2 if axis == 3 else 4):
            tk, tg = along(axis, step)
            pl.semaphore_signal(sem, inc=1, device_id={"kpt": tk, "grid": tg}, device_id_type=MESH)

    barrier = pltpu.get_barrier_semaphore()
    for axis in range(4):
        signal(barrier, axis)

    def orb_copy(plane):
        return pltpu.make_async_copy(orb.at[:, :, :, plane], obuf.at[plane], orb_sem.at[plane])

    ins = [
        pltpu.make_async_copy(tab_in, tab, in_sem.at[0]),
        pltpu.make_async_copy(row_in, rowv, in_sem.at[1]),
        pltpu.make_async_copy(lam, lamv, in_sem.at[2]),
        pltpu.make_async_copy(zb, zbuf, in_sem.at[3]),
    ]
    orb_copy(0).start()
    ins[0].start()
    for plane in range(1, PLANES):
        orb_copy(plane).start()
    for one in ins[1:]:
        one.start()

    weight = [[(kw[p] * occ[p, b]).astype(f32) * (1.0 / 64.0) for b in range(2)] for p in range(2)]

    def plane_spectrum(plane):
        orb_copy(plane).wait()
        slot = plane % 2
        for r in range(0, N, 32):
            total = None
            for p in range(2):
                for b in range(2):
                    re = obuf[plane, p, b, 0, r : r + 32, :].astype(f32)
                    im = obuf[plane, p, b, 1, r : r + 32, :].astype(f32)
                    term = weight[p][b] * (re * re + im * im)
                    total = term if total is None else total + term
            high, low = split(total)
            dh[slot, r : r + 32, :] = high
            dl[slot, r : r + 32, :] = low
        along_y = dot3(dh[slot], dl[slot], tab[0], tab[1])
        high, low = split(along_y)
        both = dot3(tab[2], tab[3], high, low)
        h, q = plane // QUAD, plane % QUAD
        for e in range(2):
            for u in range(2):
                B[h, e, pl.ds(q * 2 + u, LANES, stride=8), :] = both[
                    e * LANES : (e + 1) * LANES, u * LANES : (u + 1) * LANES
                ]

    def send_out(h, e):
        def one(step, carry):
            tk, tg = peer(step)
            pltpu.make_async_remote_copy(
                src_ref=B.at[h, e, rows_of(tk * 64 + tg, 8)],
                dst_ref=R.at[e, rows_of(me * 2 + h, 8)],
                send_sem=send_sem,
                recv_sem=recv_sem.at[e],
                device_id={"kpt": tk, "grid": tg},
                device_id_type=MESH,
            ).start()
            return carry

        lax.fori_loop(1, DEVICES, one, 0)
        R[e, rows_of(me * 2 + h, 8), :] = B[h, e, rows_of(me, 8), :]

    plane_spectrum_after = []
    ins[0].wait()
    plane_spectrum(0)
    pl.semaphore_wait(barrier, 10)
    signal(y_sem, 1)
    plane_spectrum(1)
    pl.semaphore_wait(y_sem, 3)
    signal(z_sem, 2)
    plane_spectrum(2)
    pl.semaphore_wait(z_sem, 3)
    signal(c_sem, 3)
    plane_spectrum(3)
    pl.semaphore_wait(c_sem, 1)
    send_out(0, 0)
    for plane in range(QUAD, PLANES):
        plane_spectrum(plane)
    send_out(1, 0)
    send_out(0, 1)
    send_out(1, 1)

    for one in ins[1:]:
        one.wait()
    for r in range(0, NZ, LANES):
        rows = zbuf[r : r + LANES, :]
        high, low = split(rows)
        Zh[r : r + LANES, :] = high
        Zl[r : r + LANES, :] = low
        turned = rows.T
        high, low = split(turned)
        ZhT[:, r : r + LANES] = high
        ZlT[:, r : r + LANES] = low
    shift_y, weight_y = rowv[0:1, :], rowv[1:2, :]
    lanes = lax.broadcasted_iota(jnp.int32, (1, N), 1)
    for e in range(2):
        mine = lanes == e * LANES + me
        shift_x = jnp.sum(jnp.where(mine, shift_y, 0.0), axis=1, keepdims=True)
        weight_x = jnp.sum(jnp.where(mine, weight_y, 0.0), axis=1, keepdims=True)
        for r in range(0, NZ, LANES):
            column = jnp.broadcast_to(lamv[0:1, r : r + LANES], (LANES, LANES)).T
            for u in range(2):
                cols = slice(u * LANES, (u + 1) * LANES)
                fac[e, r : r + LANES, cols] = (weight_y[:, cols] * weight_x) / (
                    column + (shift_y[:, cols] + shift_x)
                )

    def solve(e):
        taken = R.at[e, pl.ds(0, (DEVICES - 1) * 16)]
        pltpu.make_async_copy(taken, taken, recv_sem.at[e]).wait()
        for u in range(2):
            cols = slice(u * LANES, (u + 1) * LANES)
            for r in range(0, NZ, LANES):
                first = R[e, pl.ds(r * 2 + u, LANES, stride=2), :]
                second = R[e, pl.ds(1024 + r * 2 + u, LANES, stride=2), :]
                high, low = split(first + second)
                Xh[r : r + LANES, cols] = high
                Xl[r : r + LANES, cols] = low
        for r in range(0, NZ, N):
            part = dot3(ZhT[r : r + N, :], ZlT[r : r + N, :], Xh[...], Xl[...])
            high, low = split(part * fac[e, r : r + N, :])
            Yh[r : r + N, :] = high
            Yl[r : r + N, :] = low
        for r in range(0, NZ, N):
            part = dot3(Zh[r : r + N, :], Zl[r : r + N, :], Yh[...], Yl[...])
            for row in range(0, N, 8):
                for u in range(2):
                    at = (r + row) * 2 + u * 8
                    W[e, at : at + 8, :] = part[row : row + 8, u * LANES : (u + 1) * LANES]

        def one(step, carry):
            tk, tg = peer(step)
            pltpu.make_async_remote_copy(
                src_ref=W.at[e, rows_of(tg, 16)],
                dst_ref=Q.at[e, rows_of(me, 16)],
                send_sem=back_sem,
                recv_sem=got_sem.at[e],
                device_id={"kpt": tk, "grid": tg},
                device_id_type=MESH,
            ).start()
            return carry

        lax.fori_loop(1, DEVICES, one, 0)
        Q[e, rows_of(me, 16), :] = W[e, rows_of(g, 16), :]

    solve(0)
    solve(1)

    def half_done(e, plane):
        parts = [Q[e, pl.ds(u * 8 + plane, LANES, stride=16), :] for u in range(2)]
        high, low = split(jnp.concatenate(parts, axis=1))
        cols = slice(e * LANES, (e + 1) * LANES)
        return dot3(tab[0, :, cols], tab[1, :, cols], high, low)

    def arrived(e):
        taken = Q.at[e, pl.ds(0, (DEVICES - 1) * 16)]
        pltpu.make_async_copy(taken, taken, got_sem.at[e]).wait()

    arrived(0)
    for plane in range(PLANES):
        half[plane] = half_done(0, plane)
    arrived(1)
    for plane in range(PLANES):
        high, low = split(half[plane] + half_done(1, plane))
        out[plane] = dot3(high, low, tab[2], tab[3])

    sent = R.at[:, pl.ds(0, (DEVICES - 1) * 16)]
    pltpu.make_async_copy(sent, sent, send_sem).wait()
    sent = Q.at[:, pl.ds(0, (DEVICES - 1) * 16)]
    pltpu.make_async_copy(sent, sent, back_sem).wait()


def on_device(orbitals, kweights, occupations, z_basis, z_eigen):
    any_space = pl.BlockSpec(memory_space=pl.ANY)
    smem = pl.BlockSpec(memory_space=pltpu.SMEM)
    vmem = pltpu.VMEM
    dma = pltpu.SemaphoreType.DMA
    return pl.pallas_call(
        kernel,
        out_shape=jax.ShapeDtypeStruct((PLANES, N, N), f32),
        in_specs=[any_space, smem, smem, any_space, any_space, any_space, any_space],
        out_specs=pl.BlockSpec(memory_space=vmem),
        scratch_shapes=[
            vmem((PLANES, 2, 2, 2, N, N), bf16),
            vmem((NZ, NZ), f32),
            vmem((1, NZ), f32),
            vmem((4, N, N), bf16),
            vmem((8, N), f32),
            vmem((2, 2, 1024, LANES), f32),
            vmem((2, 2048, LANES), f32),
            vmem((2, 1024, LANES), f32),
            vmem((2, 2048, LANES), f32),
            vmem((NZ, NZ), bf16),
            vmem((NZ, NZ), bf16),
            vmem((NZ, NZ), bf16),
            vmem((NZ, NZ), bf16),
            vmem((2, NZ, N), f32),
            vmem((2, N, N), bf16),
            vmem((2, N, N), bf16),
            vmem((NZ, N), bf16),
            vmem((NZ, N), bf16),
            vmem((NZ, N), bf16),
            vmem((NZ, N), bf16),
            vmem((PLANES, N, N), f32),
            dma((PLANES,)),
            dma((4,)),
            dma,
            dma((2,)),
            dma,
            dma((2,)),
            pltpu.SemaphoreType.REGULAR,
            pltpu.SemaphoreType.REGULAR,
            pltpu.SemaphoreType.REGULAR,
        ],
        compiler_params=pltpu.CompilerParams(
            collective_id=0, has_side_effects=True, vmem_limit_bytes=48 << 20
        ),
    )(
        orbitals, kweights, occupations, z_basis, z_eigen.reshape(1, NZ),
        jnp.asarray(tables()), jnp.asarray(mode_rows()),
    )


def solution(mesh):
    return jax.shard_map(
        on_device,
        mesh=mesh,
        in_specs=(P("kpt", None, None, "grid", None, None), P("kpt"), P("kpt", None), P(), P()),
        out_specs=P("grid", None, None),
        check_vma=False,
    )
```

time: 138 us -> 75.1 us (0.54)
  Pallas kernels: 0 us -> 68.5 us
  waiting for transfers between devices: 61.6 us -> 0 us
  blocking collectives: 27 us -> 0 us
  starting transfers between devices: 19.9 us -> 0 us
  matrix products: 13.6 us -> 0 us
  other arithmetic: 8.38 us -> 0 us
    pallas_call x0 -> x1, Pallas kernels: none -> 68.5 us  [on_device(): pl.pallas_call(kernel, out_shape=jax.ShapeDtypeStruct((PLANES, N, N), f32...]
    all_to_all x3 -> x0, waiting for transfers between devices: 61.6 us -> none  [the longest x1 24.7 us: summed_on_arrival(): lax.all_to_all(parts, axis, split_axis=0, concat_axis=0, tiled=True)]
    all_to_all x1 -> x0, blocking collectives: 27 us -> none  [copy_for_each(): return lax.all_to_all(copies, axis, split_axis=0, concat_axis=0, tiled=True)]
    all_to_all x3 -> x0, starting transfers between devices: 19.9 us -> none  [the longest x1 11.9 us: on_device(): lax.all_to_all(spectrum, ('kpt', 'grid'), split_axis=2, concat_axis=1, ti...]
    dot_general x6 -> x0, matrix products: 13.6 us -> none  [the longest x1 2.83 us: inverse_real(): jnp.einsum('jx,zjk->zxk', scaled_x, planes[0], precision=precise)]
    reduce_sum x2 -> x0, other arithmetic: 7.45 us -> none  [the longest x1 7.22 us: on_device(): jnp.sum(factor[:, :, None, None, None, None] * values * values, axis=(0,...]
    unnamed x3 -> x13, local copies, waits for them, and re-layouts: 1.33 us -> 6.3 us
    reshape x2 -> x0, local copies, waits for them, and re-layouts: 1.89 us -> none  [the longest x1 1.53 us: on_device(): z_basis.reshape(blocks, groups, z_count, z_length).transpose(1, 0, 2, 3)]
  transfers between devices with their start and end apart: 3 -> 0, of which waited for: 3 -> 0; matrix products, arithmetic and copies ran while one was open for 2% -> 0% of each run, Pallas kernels for 0% -> 0%
where the time goes in v1:
time: 75.1 us; the launch traced here: 74.8 us
  Pallas kernels  68.5 us (91%)
  local copies, waits for them, and re-layouts  6.3 us (8%)
    pallas_call x1, Pallas kernels, on_device(): pl.pallas_call(kernel, out_shape=jax.ShapeDtypeStruct((PLANES, N, N), f32...  68.5 us
    unnamed x13, local copies, waits for them, and re-layouts  6.3 us

profile of v1, /device:TPU:1, one launch (start us, length us, event | category | flops | bytes accessed | tf_op | source)
XLA Modules:
  0.0 74.8 jit_solution(15917073082606077474)
XLA Ops:
  0.0 0.0 copy-start
  0.0 1.2 %copy-done = f32[512,512]{1,0:T(8,128)S(1)} copy-done((f32[512,512]{1,0:T(8,128)S(1)}, f32[512,512]{1,0:T(8,128)}, u32[]{:S(2)}) %copy-start) | copy-done | bytes 1048600
  1.2 0.0 copy-start.1
  1.2 1.0 %copy-done.1 = bf16[4,256,256]{2,1,0:T(8,128)(2,1)S(1)} copy-done((bf16[4,256,256]{2,1,0:T(8,128)(2,1)S(1)}, bf16[4,256,256]{2,1,0:T(8,128)(2,1)}, u32[]{:S(2)}) %copy-start.1) | copy-done | bytes 524312
  2.3 0.0 copy-start.2
  2.3 0.7 copy-done.2
  3.0 0.0 copy-start.3
  3.0 0.7 copy-done.3
  3.6 0.0 copy-start.4
  3.6 0.7 copy-done.4
  4.3 0.0 copy-start.5
  4.3 0.7 copy-done.5
  5.0 68.5 %shard_map.73 = f32[8,256,256]{2,1,0:T(8,128)S(1)} custom-call(bf16[2,2,2,8,256,256]{5,4,3,2,1,0:T(8,128)(2,1)} %orb.1, s32[2]{0:T(128)S(1)} %copy-done.5, s32[2,2]{1,0:T(2,128)S(1)} %copy-done.4, f32[512,512]{1,0:T(8,128)S(1)} %copy-done, f32[1,512]{1,0:T(1,128)S(1)} %bitcast.1, bf16[4,256,256]{2,1,0:T(8,128)(2,1)S(1)} %copy-done.1, f32[8,256]{1,0:T(8,128)S(1)} %copy-done.2), custom_call_target="tpu_custom_call" | custom-call | tf_op jit(solution)/shard_map/pallas_call | solution.py:288
  73.5 1.3 %copy.9 = f32[8,256,256]{2,1,0:T(8,128)} copy(f32[8,256,256]{2,1,0:T(8,128)S(1)} %shard_map.73) | data formatting | bytes 4194304
Async XLA Ops:
  0.0 1.2 %copy-start = (f32[512,512]{1,0:T(8,128)S(1)}, f32[512,512]{1,0:T(8,128)}, u32[]{:S(2)}) copy-start(f32[512,512]{1,0:T(8,128)} %zb.1) | copy-start | bytes 3145732
  1.2 1.0 %copy-start.1 = (bf16[4,256,256]{2,1,0:T(8,128)(2,1)S(1)}, bf16[4,256,256]{2,1,0:T(8,128)(2,1)}, u32[]{:S(2)}) copy-start(bf16[4,256,256]{2,1,0:T(8,128)(2,1)} %constant.4.clone.tab_in) | copy-start | bytes 1572868
  2.3 0.7 copy-start.2
  3.0 0.7 copy-start.3
  3.6 0.7 copy-start.4
  4.3 0.7 copy-start.5

commit v2 on v1

--- a/solution.py
+++ b/solution.py
@@ -69,15 +69,25 @@
     return lax.rem(x, 2), ((x // 2 * 4 + z) * 4 + y) * 2 + c
 
 
-def peer(step):
+def for_each_peer(act):
     x, y, z, c = coords()
-    mixed = lax.rem(step * 37, 128)
-    return device(
-        lax.rem(x + lax.rem(mixed, 4), 4),
-        lax.rem(y + lax.rem(mixed // 4, 4), 4),
-        lax.rem(z + lax.rem(mixed // 16, 4), 4),
-        lax.rem(c + mixed // 64, 2),
-    )
+    across = []
+    for step in (1, 3, 2, 0):
+        tx = lax.rem(x + step, 4)
+        for flip in range(2):
+            across.append((lax.rem(tx, 2), tx // 2 * 32 + lax.rem(c + flip, 2)))
+
+    def block(dy, dz, chosen):
+        base = lax.rem(z + dz, 4) * 8 + lax.rem(y + dy, 4) * 2
+        for tk, part in chosen:
+            act(tk, base + part)
+
+    def one(index, carry):
+        block(lax.rem(index, 4), index // 4, across)
+        return carry
+
+    lax.fori_loop(1, 16, one, 0)
+    block(0, 0, across[:6] + across[7:])
 
 
 def rows_of(index, count):
@@ -85,32 +95,27 @@
 
 
 def kernel(
-    orb, kw, occ, zb, lam, tab_in, row_in, out,
-    obuf, zbuf, lamv, tab, rowv, B, R, W, Q, Zh, Zl, ZhT, ZlT, fac,
+    orb, kw_in, occ_in, zb, lam, tab_in, row_in, out,
+    kwv, occv, obuf, zbuf, lamv, tab, rowv, B, R, W, Q, Zh, Zl, ZhT, ZlT, fac,
     dh, dl, Xh, Xl, Yh, Yl, half,
-    orb_sem, in_sem, send_sem, recv_sem, back_sem, got_sem, y_sem, z_sem, c_sem,
+    orb_sem, in_sem, send_sem, recv_sem, back_sem, got_sem, column_sem,
 ):
     k = lax.axis_index("kpt")
     g = lax.axis_index("grid")
     me = k * 64 + g
     x, y, z, c = coords()
 
-    def along(axis, step):
-        return device(
-            lax.rem(x + step, 4) if axis == 0 else x,
-            lax.rem(y + step, 4) if axis == 1 else y,
-            lax.rem(z + step, 4) if axis == 2 else z,
-            lax.rem(c + step, 2) if axis == 3 else c,
-        )
-
-    def signal(sem, axis):
-        for step in range(1, 2 if axis == 3 else 4):
-            tk, tg = along(axis, step)
+    def signal(sem, steps):
+        for dx, dy, dz, dc in steps:
+            tk, tg = device(
+                lax.rem(x + dx, 4), lax.rem(y + dy, 4), lax.rem(z + dz, 4), lax.rem(c + dc, 2)
+            )
             pl.semaphore_signal(sem, inc=1, device_id={"kpt": tk, "grid": tg}, device_id_type=MESH)
 
+    plane_steps = [(i % 4, i // 4, 0, 0) for i in range(1, 16)]
+    column_steps = [(0, 0, i % 4, i // 4) for i in range(1, 8)]
     barrier = pltpu.get_barrier_semaphore()
-    for axis in range(4):
-        signal(barrier, axis)
+    signal(barrier, plane_steps + column_steps)
 
     def orb_copy(plane):
         return pltpu.make_async_copy(orb.at[:, :, :, plane], obuf.at[plane], orb_sem.at[plane])
@@ -121,6 +126,12 @@
         pltpu.make_async_copy(lam, lamv, in_sem.at[2]),
         pltpu.make_async_copy(zb, zbuf, in_sem.at[3]),
     ]
+    scalars = [
+        pltpu.make_async_copy(kw_in, kwv, in_sem.at[4]),
+        pltpu.make_async_copy(occ_in, occv, in_sem.at[5]),
+    ]
+    for one in scalars:
+        one.start()
     orb_copy(0).start()
     ins[0].start()
     for plane in range(1, PLANES):
@@ -128,7 +139,9 @@
     for one in ins[1:]:
         one.start()
 
-    weight = [[(kw[p] * occ[p, b]).astype(f32) * (1.0 / 64.0) for b in range(2)] for p in range(2)]
+    for one in scalars:
+        one.wait()
+    weight = [[(kwv[p] * occv[p, b]).astype(f32) * (1.0 / 64.0) for b in range(2)] for p in range(2)]
 
     def plane_spectrum(plane):
         orb_copy(plane).wait()
@@ -155,8 +168,7 @@
                 ]
 
     def send_out(h, e):
-        def one(step, carry):
-            tk, tg = peer(step)
+        def act(tk, tg):
             pltpu.make_async_remote_copy(
                 src_ref=B.at[h, e, rows_of(tk * 64 + tg, 8)],
                 dst_ref=R.at[e, rows_of(me * 2 + h, 8)],
@@ -165,24 +177,18 @@
                 device_id={"kpt": tk, "grid": tg},
                 device_id_type=MESH,
             ).start()
-            return carry
-
-        lax.fori_loop(1, DEVICES, one, 0)
+
+        for_each_peer(act)
         R[e, rows_of(me * 2 + h, 8), :] = B[h, e, rows_of(me, 8), :]
 
-    plane_spectrum_after = []
     ins[0].wait()
     plane_spectrum(0)
-    pl.semaphore_wait(barrier, 10)
-    signal(y_sem, 1)
     plane_spectrum(1)
-    pl.semaphore_wait(y_sem, 3)
-    signal(z_sem, 2)
+    pl.semaphore_wait(barrier, 22)
+    signal(column_sem, column_steps)
     plane_spectrum(2)
-    pl.semaphore_wait(z_sem, 3)
-    signal(c_sem, 3)
     plane_spectrum(3)
-    pl.semaphore_wait(c_sem, 1)
+    pl.semaphore_wait(column_sem, 7)
     send_out(0, 0)
     for plane in range(QUAD, PLANES):
         plane_spectrum(plane)
@@ -215,6 +221,8 @@
                     column + (shift_y[:, cols] + shift_x)
                 )
 
+    upper = lax.broadcasted_iota(jnp.int32, (8, LANES), 0) < QUAD
+
     def solve(e):
         taken = R.at[e, pl.ds(0, (DEVICES - 1) * 16)]
         pltpu.make_async_copy(taken, taken, recv_sem.at[e]).wait()
@@ -234,63 +242,68 @@
         for r in range(0, NZ, N):
             part = dot3(Zh[r : r + N, :], Zl[r : r + N, :], Yh[...], Yl[...])
             for row in range(0, N, 8):
-                for u in range(2):
-                    at = (r + row) * 2 + u * 8
-                    W[e, at : at + 8, :] = part[row : row + 8, u * LANES : (u + 1) * LANES]
-
-        def one(step, carry):
-            tk, tg = peer(step)
+                first = part[row : row + 8, :LANES]
+                second = part[row : row + 8, LANES:]
+                at = slice(r + row, r + row + 8)
+                W[e, 0, at, :] = jnp.where(upper, first, pltpu.roll(second, QUAD, 0))
+                W[e, 1, at, :] = jnp.where(upper, pltpu.roll(first, QUAD, 0), second)
+
+    def send_back(e, h):
+        def act(tk, tg):
             pltpu.make_async_remote_copy(
-                src_ref=W.at[e, rows_of(tg, 16)],
-                dst_ref=Q.at[e, rows_of(me, 16)],
+                src_ref=W.at[e, h, rows_of(tg, 8)],
+                dst_ref=Q.at[e, h, rows_of(me, 8)],
                 send_sem=back_sem,
-                recv_sem=got_sem.at[e],
+                recv_sem=got_sem.at[e + h * e],
                 device_id={"kpt": tk, "grid": tg},
                 device_id_type=MESH,
             ).start()
-            return carry
-
-        lax.fori_loop(1, DEVICES, one, 0)
-        Q[e, rows_of(me, 16), :] = W[e, rows_of(g, 16), :]
+
+        for_each_peer(act)
+        Q[e, h, rows_of(me, 8), :] = W[e, h, rows_of(g, 8), :]
 
     solve(0)
+    send_back(0, 0)
+    send_back(0, 1)
     solve(1)
+    send_back(1, 0)
+    send_back(1, 1)
 
     def half_done(e, plane):
-        parts = [Q[e, pl.ds(u * 8 + plane, LANES, stride=16), :] for u in range(2)]
+        h, q = plane // QUAD, plane % QUAD
+        parts = [Q[e, h, pl.ds(u * QUAD + q, LANES, stride=8), :] for u in range(2)]
         high, low = split(jnp.concatenate(parts, axis=1))
         cols = slice(e * LANES, (e + 1) * LANES)
         return dot3(tab[0, :, cols], tab[1, :, cols], high, low)
 
-    def arrived(e):
-        taken = Q.at[e, pl.ds(0, (DEVICES - 1) * 16)]
-        pltpu.make_async_copy(taken, taken, got_sem.at[e]).wait()
-
-    arrived(0)
+    def arrived(taken, sem):
+        pltpu.make_async_copy(taken, taken, sem).wait()
+
+    arrived(Q.at[0, :, pl.ds(0, (DEVICES - 1) * 8)], got_sem.at[0])
     for plane in range(PLANES):
         half[plane] = half_done(0, plane)
-    arrived(1)
-    for plane in range(PLANES):
-        high, low = split(half[plane] + half_done(1, plane))
-        out[plane] = dot3(high, low, tab[2], tab[3])
-
-    sent = R.at[:, pl.ds(0, (DEVICES - 1) * 16)]
-    pltpu.make_async_copy(sent, sent, send_sem).wait()
-    sent = Q.at[:, pl.ds(0, (DEVICES - 1) * 16)]
-    pltpu.make_async_copy(sent, sent, back_sem).wait()
+    for h in range(2):
+        arrived(Q.at[1, h, pl.ds(0, (DEVICES - 1) * 8)], got_sem.at[1 + h])
+        for plane in range(h * QUAD, (h + 1) * QUAD):
+            high, low = split(half[plane] + half_done(1, plane))
+            out[plane] = dot3(high, low, tab[2], tab[3])
+
+    arrived(R.at[:, pl.ds(0, (DEVICES - 1) * 16)], send_sem)
+    arrived(Q.at[:, :, pl.ds(0, (DEVICES - 1) * 8)], back_sem)
 
 
 def on_device(orbitals, kweights, occupations, z_basis, z_eigen):
-    any_space = pl.BlockSpec(memory_space=pl.ANY)
-    smem = pl.BlockSpec(memory_space=pltpu.SMEM)
+    hbm = pl.BlockSpec(memory_space=pltpu.HBM)
     vmem = pltpu.VMEM
     dma = pltpu.SemaphoreType.DMA
     return pl.pallas_call(
         kernel,
         out_shape=jax.ShapeDtypeStruct((PLANES, N, N), f32),
-        in_specs=[any_space, smem, smem, any_space, any_space, any_space, any_space],
+        in_specs=[hbm] * 7,
         out_specs=pl.BlockSpec(memory_space=vmem),
         scratch_shapes=[
+            pltpu.SMEM((2,), jnp.int32),
+            pltpu.SMEM((2, 2), jnp.int32),
             vmem((PLANES, 2, 2, 2, N, N), bf16),
             vmem((NZ, NZ), f32),
             vmem((1, NZ), f32),
@@ -298,8 +311,8 @@
             vmem((8, N), f32),
             vmem((2, 2, 1024, LANES), f32),
             vmem((2, 2048, LANES), f32),
-            vmem((2, 1024, LANES), f32),
-            vmem((2, 2048, LANES), f32),
+            vmem((2, 2, 512, LANES), f32),
+            vmem((2, 2, 1024, LANES), f32),
             vmem((NZ, NZ), bf16),
             vmem((NZ, NZ), bf16),
             vmem((NZ, NZ), bf16),
@@ -313,22 +326,20 @@
             vmem((NZ, N), bf16),
             vmem((PLANES, N, N), f32),
             dma((PLANES,)),
-            dma((4,)),
+            dma((6,)),
             dma,
             dma((2,)),
             dma,
-            dma((2,)),
-            pltpu.SemaphoreType.REGULAR,
-            pltpu.SemaphoreType.REGULAR,
+            dma((3,)),
             pltpu.SemaphoreType.REGULAR,
         ],
         compiler_params=pltpu.CompilerParams(
             collective_id=0, has_side_effects=True, vmem_limit_bytes=48 << 20
         ),
-    )(
+    )(*(pltpu.with_memory_space_constraint(one, pltpu.HBM) for one in (
         orbitals, kweights, occupations, z_basis, z_eigen.reshape(1, NZ),
         jnp.asarray(tables()), jnp.asarray(mode_rows()),
-    )
+    )))
 
 
 def solution(mesh):

time: 75.1 us -> 64.3 us (0.86)
  Pallas kernels: 68.5 us -> 62.9 us
  local copies, waits for them, and re-layouts: 6.3 us -> 1.32 us
    pallas_call x1, Pallas kernels: 68.5 us -> 62.9 us  [on_device(): pl.pallas_call(kernel, out_shape=jax.ShapeDtypeStruct((PLANES, N, N), f32...]
    unnamed x13 -> x1, local copies, waits for them, and re-layouts: 6.3 us -> 1.32 us
where the time goes in v2:
time: 64.3 us; the launch traced here: 64.2 us
  Pallas kernels  62.9 us (98%)
  local copies, waits for them, and re-layouts  1.32 us (2%)
    pallas_call x1, Pallas kernels, on_device(): pl.pallas_call(kernel, out_shape=jax.ShapeDtypeStruct((PLANES, N, N), f32...  62.9 us
    unnamed x1, local copies, waits for them, and re-layouts  1.32 us

profile of v2, /device:TPU:1, one launch (start us, length us, event | category | flops | bytes accessed | tf_op | source)
XLA Modules:
  0.0 64.2 jit_solution(11994754581071219766)
XLA Ops:
  0.0 62.9 %shard_map.73 = f32[8,256,256]{2,1,0:T(8,128)S(1)} custom-call(bf16[2,2,2,8,256,256]{5,4,3,2,1,0:T(8,128)(2,1)} %orb.1, s32[2]{0:T(128)} %kw_in.1, s32[2,2]{1,0:T(2,128)} %occ_in.1, f32[512,512]{1,0:T(8,128)} %zb.1, f32[1,512]{1,0:T(1,128)} %bitcast.1, bf16[4,256,256]{2,1,0:T(8,128)(2,1)} %constant.4.clone.tab_in, f32[8,256]{1,0:T(8,128)} %constant.5.clone.row_in), custom_call_target="tpu_custom_call" | custom-call | tf_op jit(solution)/shard_map/pallas_call | solution.py:299
  62.9 1.3 %copy.9 = f32[8,256,256]{2,1,0:T(8,128)} copy(f32[8,256,256]{2,1,0:T(8,128)S(1)} %shard_map.73) | data formatting | bytes 4194304

commit v3 on v2

--- a/solution.py
+++ b/solution.py
@@ -96,9 +96,9 @@
 
 def kernel(
     orb, kw_in, occ_in, zb, lam, tab_in, row_in, out,
-    kwv, occv, obuf, zbuf, lamv, tab, rowv, B, R, W, Q, Zh, Zl, ZhT, ZlT, fac,
-    dh, dl, Xh, Xl, Yh, Yl, half,
-    orb_sem, in_sem, send_sem, recv_sem, back_sem, got_sem, column_sem,
+    kwv, occv, obuf, zbuf, lamv, to_ky, to_jx, from_jx, from_ky, rowv, B, R, W, Q, Zh, Zl, ZhT, ZlT, fac,
+    dcat, ecat, Xh, Xl, Yh, Yl, half, fcat, acat,
+    orb_sem, in_sem, tab_sem, send_sem, recv_sem, back_sem, got_sem, column_sem,
 ):
     k = lax.axis_index("kpt")
     g = lax.axis_index("grid")
@@ -121,7 +121,6 @@
         return pltpu.make_async_copy(orb.at[:, :, :, plane], obuf.at[plane], orb_sem.at[plane])
 
     ins = [
-        pltpu.make_async_copy(tab_in, tab, in_sem.at[0]),
         pltpu.make_async_copy(row_in, rowv, in_sem.at[1]),
         pltpu.make_async_copy(lam, lamv, in_sem.at[2]),
         pltpu.make_async_copy(zb, zbuf, in_sem.at[3]),
@@ -132,11 +131,29 @@
     ]
     for one in scalars:
         one.start()
+
+    def table_copies(lo, hi):
+        sources = [tab_in.at[0], tab_in.at[1], tab_in.at[0], tab_in.at[2], tab_in.at[2], tab_in.at[3]]
+        sources += [
+            tab_in.at[part, :, e * LANES : (e + 1) * LANES] for e in range(2) for part in (0, 0, 1)
+        ]
+        sources += [tab_in.at[2], tab_in.at[3], tab_in.at[2]]
+        targets = [to_ky.at[i * N : (i + 1) * N] for i in range(3)]
+        targets += [to_jx.at[:, i * N : (i + 1) * N] for i in range(3)]
+        targets += [
+            from_jx.at[e, :, i * LANES : (i + 1) * LANES] for e in range(2) for i in range(3)
+        ]
+        targets += [from_ky.at[i * N : (i + 1) * N] for i in range(3)]
+        return [
+            pltpu.make_async_copy(sources[i], targets[i], tab_sem.at[i]) for i in range(lo, hi)
+        ]
+
     orb_copy(0).start()
-    ins[0].start()
+    for one in table_copies(0, 6):
+        one.start()
     for plane in range(1, PLANES):
         orb_copy(plane).start()
-    for one in ins[1:]:
+    for one in table_copies(6, 15) + ins:
         one.start()
 
     for one in scalars:
@@ -155,11 +172,17 @@
                     term = weight[p][b] * (re * re + im * im)
                     total = term if total is None else total + term
             high, low = split(total)
-            dh[slot, r : r + 32, :] = high
-            dl[slot, r : r + 32, :] = low
-        along_y = dot3(dh[slot], dl[slot], tab[0], tab[1])
-        high, low = split(along_y)
-        both = dot3(tab[2], tab[3], high, low)
+            dcat[slot, r : r + 32, 0:N] = high
+            dcat[slot, r : r + 32, N : 2 * N] = high
+            dcat[slot, r : r + 32, 2 * N : 3 * N] = low
+        if plane == 0:
+            for one in table_copies(0, 6):
+                one.wait()
+        high, low = split(dot(dcat[slot], to_ky[...]))
+        ecat[slot, 0:N, :] = high
+        ecat[slot, N : 2 * N, :] = low
+        ecat[slot, 2 * N : 3 * N, :] = high
+        both = dot(to_jx[...], ecat[slot])
         h, q = plane // QUAD, plane % QUAD
         for e in range(2):
             for u in range(2):
@@ -181,11 +204,10 @@
         for_each_peer(act)
         R[e, rows_of(me * 2 + h, 8), :] = B[h, e, rows_of(me, 8), :]
 
-    ins[0].wait()
     plane_spectrum(0)
-    plane_spectrum(1)
     pl.semaphore_wait(barrier, 22)
     signal(column_sem, column_steps)
+    plane_spectrum(1)
     plane_spectrum(2)
     plane_spectrum(3)
     pl.semaphore_wait(column_sem, 7)
@@ -196,7 +218,7 @@
     send_out(0, 1)
     send_out(1, 1)
 
-    for one in ins[1:]:
+    for one in table_copies(6, 15) + ins:
         one.wait()
     for r in range(0, NZ, LANES):
         rows = zbuf[r : r + LANES, :]
@@ -273,8 +295,11 @@
         h, q = plane // QUAD, plane % QUAD
         parts = [Q[e, h, pl.ds(u * QUAD + q, LANES, stride=8), :] for u in range(2)]
         high, low = split(jnp.concatenate(parts, axis=1))
-        cols = slice(e * LANES, (e + 1) * LANES)
-        return dot3(tab[0, :, cols], tab[1, :, cols], high, low)
+        slot = plane % 2
+        fcat[slot, 0:LANES, :] = high
+        fcat[slot, LANES : 2 * LANES, :] = low
+        fcat[slot, 2 * LANES : 3 * LANES, :] = high
+        return dot(from_jx[e], fcat[slot])
 
     def arrived(taken, sem):
         pltpu.make_async_copy(taken, taken, sem).wait()
@@ -286,7 +311,11 @@
         arrived(Q.at[1, h, pl.ds(0, (DEVICES - 1) * 8)], got_sem.at[1 + h])
         for plane in range(h * QUAD, (h + 1) * QUAD):
             high, low = split(half[plane] + half_done(1, plane))
-            out[plane] = dot3(high, low, tab[2], tab[3])
+            slot = plane % 2
+            acat[slot, :, 0:N] = high
+            acat[slot, :, N : 2 * N] = high
+            acat[slot, :, 2 * N : 3 * N] = low
+            out[plane] = dot(acat[slot], from_ky[...])
 
     arrived(R.at[:, pl.ds(0, (DEVICES - 1) * 16)], send_sem)
     arrived(Q.at[:, :, pl.ds(0, (DEVICES - 1) * 8)], back_sem)
@@ -307,7 +336,10 @@
             vmem((PLANES, 2, 2, 2, N, N), bf16),
             vmem((NZ, NZ), f32),
             vmem((1, NZ), f32),
-            vmem((4, N, N), bf16),
+            vmem((3 * N, N), bf16),
+            vmem((N, 3 * N), bf16),
+            vmem((2, N, 3 * LANES), bf16),
+            vmem((3 * N, N), bf16),
             vmem((8, N), f32),
             vmem((2, 2, 1024, LANES), f32),
             vmem((2, 2048, LANES), f32),
@@ -318,15 +350,18 @@
             vmem((NZ, NZ), bf16),
             vmem((NZ, NZ), bf16),
             vmem((2, NZ, N), f32),
-            vmem((2, N, N), bf16),
-            vmem((2, N, N), bf16),
+            vmem((2, N, 3 * N), bf16),
+            vmem((2, 3 * N, N), bf16),
             vmem((NZ, N), bf16),
             vmem((NZ, N), bf16),
             vmem((NZ, N), bf16),
             vmem((NZ, N), bf16),
             vmem((PLANES, N, N), f32),
+            vmem((2, 3 * LANES, N), bf16),
+            vmem((2, N, 3 * N), bf16),
             dma((PLANES,)),
             dma((6,)),
+            dma((15,)),
             dma,
             dma((2,)),
             dma,

time: 64.3 us -> 63 us (0.980)
  Pallas kernels: 62.9 us -> 61.6 us
    pallas_call x1, Pallas kernels: 62.9 us -> 61.6 us  [on_device(): pl.pallas_call(kernel, out_shape=jax.ShapeDtypeStruct((PLANES, N, N), f32...]
where the time goes in v3:
time: 63 us; the launch traced here: 62.9 us
  Pallas kernels  61.6 us (98%)
  local copies, waits for them, and re-layouts  1.32 us (2%)
    pallas_call x1, Pallas kernels, on_device(): pl.pallas_call(kernel, out_shape=jax.ShapeDtypeStruct((PLANES, N, N), f32...  61.6 us
    unnamed x1, local copies, waits for them, and re-layouts  1.32 us

profile of v3, /device:TPU:1, one launch (start us, length us, event | category | flops | bytes accessed | tf_op | source)
XLA Modules:
  0.0 62.9 jit_solution(18228934830053992413)
XLA Ops:
  0.0 61.6 %shard_map.73 = f32[8,256,256]{2,1,0:T(8,128)S(1)} custom-call(bf16[2,2,2,8,256,256]{5,4,3,2,1,0:T(8,128)(2,1)} %orb.1, s32[2]{0:T(128)} %kw_in.1, s32[2,2]{1,0:T(2,128)} %occ_in.1, f32[512,512]{1,0:T(8,128)} %zb.1, f32[1,512]{1,0:T(1,128)} %bitcast.1, bf16[4,256,256]{2,1,0:T(8,128)(2,1)} %constant.4.clone.tab_in, f32[8,256]{1,0:T(8,128)} %constant.5.clone.row_in), custom_call_target="tpu_custom_call" | custom-call | tf_op jit(solution)/shard_map/pallas_call | solution.py:328
  61.6 1.3 %copy.9 = f32[8,256,256]{2,1,0:T(8,128)} copy(f32[8,256,256]{2,1,0:T(8,128)S(1)} %shard_map.73) | data formatting | bytes 4194304

commit v4 on v3

--- a/solution.py
+++ b/solution.py
@@ -97,7 +97,7 @@
 def kernel(
     orb, kw_in, occ_in, zb, lam, tab_in, row_in, out,
     kwv, occv, obuf, zbuf, lamv, to_ky, to_jx, from_jx, from_ky, rowv, B, R, W, Q, Zh, Zl, ZhT, ZlT, fac,
-    dcat, ecat, Xh, Xl, Yh, Yl, half, fcat, acat,
+    density, Xh, Xl, Yh, Yl, half, fcat, acat,
     orb_sem, in_sem, tab_sem, send_sem, recv_sem, back_sem, got_sem, column_sem,
 ):
     k = lax.axis_index("kpt")
@@ -133,13 +133,12 @@
         one.start()
 
     def table_copies(lo, hi):
-        sources = [tab_in.at[0], tab_in.at[1], tab_in.at[0], tab_in.at[2], tab_in.at[2], tab_in.at[3]]
+        sources = [tab_in.at[0], tab_in.at[1], tab_in.at[2], tab_in.at[3]]
         sources += [
             tab_in.at[part, :, e * LANES : (e + 1) * LANES] for e in range(2) for part in (0, 0, 1)
         ]
         sources += [tab_in.at[2], tab_in.at[3], tab_in.at[2]]
-        targets = [to_ky.at[i * N : (i + 1) * N] for i in range(3)]
-        targets += [to_jx.at[:, i * N : (i + 1) * N] for i in range(3)]
+        targets = [to_ky.at[0], to_ky.at[1], to_jx.at[0], to_jx.at[1]]
         targets += [
             from_jx.at[e, :, i * LANES : (i + 1) * LANES] for e in range(2) for i in range(3)
         ]
@@ -149,11 +148,11 @@
         ]
 
     orb_copy(0).start()
-    for one in table_copies(0, 6):
+    for one in table_copies(0, 4):
         one.start()
     for plane in range(1, PLANES):
         orb_copy(plane).start()
-    for one in table_copies(6, 15) + ins:
+    for one in table_copies(4, 13) + ins:
         one.start()
 
     for one in scalars:
@@ -172,17 +171,13 @@
                     term = weight[p][b] * (re * re + im * im)
                     total = term if total is None else total + term
             high, low = split(total)
-            dcat[slot, r : r + 32, 0:N] = high
-            dcat[slot, r : r + 32, N : 2 * N] = high
-            dcat[slot, r : r + 32, 2 * N : 3 * N] = low
+            density[slot, 0, r : r + 32, :] = high
+            density[slot, 1, r : r + 32, :] = low
         if plane == 0:
-            for one in table_copies(0, 6):
+            for one in table_copies(0, 4):
                 one.wait()
-        high, low = split(dot(dcat[slot], to_ky[...]))
-        ecat[slot, 0:N, :] = high
-        ecat[slot, N : 2 * N, :] = low
-        ecat[slot, 2 * N : 3 * N, :] = high
-        both = dot(to_jx[...], ecat[slot])
+        high, low = split(dot3(density[slot, 0], density[slot, 1], to_ky[0], to_ky[1]))
+        both = dot3(to_jx[0], to_jx[1], high, low)
         h, q = plane // QUAD, plane % QUAD
         for e in range(2):
             for u in range(2):
@@ -218,7 +213,7 @@
     send_out(0, 1)
     send_out(1, 1)
 
-    for one in table_copies(6, 15) + ins:
+    for one in table_copies(4, 13) + ins:
         one.wait()
     for r in range(0, NZ, LANES):
         rows = zbuf[r : r + LANES, :]
@@ -311,11 +306,11 @@
         arrived(Q.at[1, h, pl.ds(0, (DEVICES - 1) * 8)], got_sem.at[1 + h])
         for plane in range(h * QUAD, (h + 1) * QUAD):
             high, low = split(half[plane] + half_done(1, plane))
-            slot = plane % 2
-            acat[slot, :, 0:N] = high
-            acat[slot, :, N : 2 * N] = high
-            acat[slot, :, 2 * N : 3 * N] = low
-            out[plane] = dot(acat[slot], from_ky[...])
+            at = slice(plane % QUAD * N, (plane % QUAD + 1) * N)
+            acat[at, 0:N] = high
+            acat[at, N : 2 * N] = high
+            acat[at, 2 * N : 3 * N] = low
+        out[h * QUAD : (h + 1) * QUAD] = dot(acat[...], from_ky[...]).reshape(QUAD, N, N)
 
     arrived(R.at[:, pl.ds(0, (DEVICES - 1) * 16)], send_sem)
     arrived(Q.at[:, :, pl.ds(0, (DEVICES - 1) * 8)], back_sem)
@@ -336,8 +331,8 @@
             vmem((PLANES, 2, 2, 2, N, N), bf16),
             vmem((NZ, NZ), f32),
             vmem((1, NZ), f32),
-            vmem((3 * N, N), bf16),
-            vmem((N, 3 * N), bf16),
+            vmem((2, N, N), bf16),
+            vmem((2, N, N), bf16),
             vmem((2, N, 3 * LANES), bf16),
             vmem((3 * N, N), bf16),
             vmem((8, N), f32),
@@ -350,18 +345,17 @@
             vmem((NZ, NZ), bf16),
             vmem((NZ, NZ), bf16),
             vmem((2, NZ, N), f32),
-            vmem((2, N, 3 * N), bf16),
-            vmem((2, 3 * N, N), bf16),
+            vmem((2, 2, N, N), bf16),
             vmem((NZ, N), bf16),
             vmem((NZ, N), bf16),
             vmem((NZ, N), bf16),
             vmem((NZ, N), bf16),
             vmem((PLANES, N, N), f32),
             vmem((2, 3 * LANES, N), bf16),
-            vmem((2, N, 3 * N), bf16),
+            vmem((QUAD * N, 3 * N), bf16),
             dma((PLANES,)),
             dma((6,)),
-            dma((15,)),
+            dma((13,)),
             dma,
             dma((2,)),
             dma,

time: 63 us -> 62.5 us (level)
  no operation moved by 1% of the time
where the time goes in v4:
time: 62.5 us; the launch traced here: 62.4 us
  Pallas kernels  61.1 us (98%)
  local copies, waits for them, and re-layouts  1.32 us (2%)
    pallas_call x1, Pallas kernels, on_device(): pl.pallas_call(kernel, out_shape=jax.ShapeDtypeStruct((PLANES, N, N), f32...  61.1 us
    unnamed x1, local copies, waits for them, and re-layouts  1.32 us

profile of v4, /device:TPU:1, one launch (start us, length us, event | category | flops | bytes accessed | tf_op | source)
XLA Modules:
  0.0 62.4 jit_solution(7622421207292959270)
XLA Ops:
  0.0 61.1 %shard_map.73 = f32[8,256,256]{2,1,0:T(8,128)S(1)} custom-call(bf16[2,2,2,8,256,256]{5,4,3,2,1,0:T(8,128)(2,1)} %orb.1, s32[2]{0:T(128)} %kw_in.1, s32[2,2]{1,0:T(2,128)} %occ_in.1, f32[512,512]{1,0:T(8,128)} %zb.1, f32[1,512]{1,0:T(1,128)} %bitcast.1, bf16[4,256,256]{2,1,0:T(8,128)(2,1)} %constant.4.clone.tab_in, f32[8,256]{1,0:T(8,128)} %constant.5.clone.row_in), custom_call_target="tpu_custom_call" | custom-call | tf_op jit(solution)/shard_map/pallas_call | solution.py:323
  61.1 1.3 %copy.9 = f32[8,256,256]{2,1,0:T(8,128)} copy(f32[8,256,256]{2,1,0:T(8,128)S(1)} %shard_map.73) | data formatting | bytes 4194304

commit v5 on v4

--- a/solution.py
+++ b/solution.py
@@ -75,12 +75,12 @@
     for step in (1, 3, 2, 0):
         tx = lax.rem(x + step, 4)
         for flip in range(2):
-            across.append((lax.rem(tx, 2), tx // 2 * 32 + lax.rem(c + flip, 2)))
+            across.append((step, lax.rem(tx, 2), tx // 2 * 32 + lax.rem(c + flip, 2)))
 
     def block(dy, dz, chosen):
-        base = lax.rem(z + dz, 4) * 8 + lax.rem(y + dy, 4) * 2
-        for tk, part in chosen:
-            act(tk, base + part)
+        base = [lax.rem(z + dz + dx, 4) * 8 + lax.rem(y + dy + dx, 4) * 2 for dx in range(4)]
+        for step, tk, part in chosen:
+            act(tk, base[step] + part)
 
     def one(index, carry):
         block(lax.rem(index, 4), index // 4, across)
@@ -207,10 +207,10 @@
     plane_spectrum(3)
     pl.semaphore_wait(column_sem, 7)
     send_out(0, 0)
+    send_out(0, 1)
     for plane in range(QUAD, PLANES):
         plane_spectrum(plane)
     send_out(1, 0)
-    send_out(0, 1)
     send_out(1, 1)
 
     for one in table_copies(4, 13) + ins:

time: 62.5 us -> 65.5 us (1.048)
  Pallas kernels: 61.1 us -> 64.1 us
    pallas_call x1, Pallas kernels: 61.1 us -> 64.1 us  [on_device(): pl.pallas_call(kernel, out_shape=jax.ShapeDtypeStruct((PLANES, N, N), f32...]
where the time goes in v5:
time: 65.5 us; the launch traced here: 65.4 us
  Pallas kernels  64.1 us (98%)
  local copies, waits for them, and re-layouts  1.32 us (2%)
    pallas_call x1, Pallas kernels, on_device(): pl.pallas_call(kernel, out_shape=jax.ShapeDtypeStruct((PLANES, N, N), f32...  64.1 us
    unnamed x1, local copies, waits for them, and re-layouts  1.32 us

profile of v5, /device:TPU:1, one launch (start us, length us, event | category | flops | bytes accessed | tf_op | source)
XLA Modules:
  0.0 65.4 jit_solution(16220098469378287878)
XLA Ops:
  0.0 64.1 %shard_map.73 = f32[8,256,256]{2,1,0:T(8,128)S(1)} custom-call(bf16[2,2,2,8,256,256]{5,4,3,2,1,0:T(8,128)(2,1)} %orb.1, s32[2]{0:T(128)} %kw_in.1, s32[2,2]{1,0:T(2,128)} %occ_in.1, f32[512,512]{1,0:T(8,128)} %zb.1, f32[1,512]{1,0:T(1,128)} %bitcast.1, bf16[4,256,256]{2,1,0:T(8,128)(2,1)} %constant.4.clone.tab_in, f32[8,256]{1,0:T(8,128)} %constant.5.clone.row_in), custom_call_target="tpu_custom_call" | custom-call | tf_op jit(solution)/shard_map/pallas_call | solution.py:323
  64.1 1.3 %copy.9 = f32[8,256,256]{2,1,0:T(8,128)} copy(f32[8,256,256]{2,1,0:T(8,128)S(1)} %shard_map.73) | data formatting | bytes 4194304

commit v6 on v4

--- a/solution.py
+++ b/solution.py
@@ -207,10 +207,10 @@
     plane_spectrum(3)
     pl.semaphore_wait(column_sem, 7)
     send_out(0, 0)
+    send_out(0, 1)
     for plane in range(QUAD, PLANES):
         plane_spectrum(plane)
     send_out(1, 0)
-    send_out(0, 1)
     send_out(1, 1)
 
     for one in table_copies(4, 13) + ins:

time: 62.5 us -> 63.4 us (1.014)
  Pallas kernels: 61.1 us -> 61.9 us
    pallas_call x1, Pallas kernels: 61.1 us -> 61.9 us  [on_device(): pl.pallas_call(kernel, out_shape=jax.ShapeDtypeStruct((PLANES, N, N), f32...]
where the time goes in v6:
time: 63.4 us; the launch traced here: 63.3 us
  Pallas kernels  61.9 us (98%)
  local copies, waits for them, and re-layouts  1.32 us (2%)
    pallas_call x1, Pallas kernels, on_device(): pl.pallas_call(kernel, out_shape=jax.ShapeDtypeStruct((PLANES, N, N), f32...  61.9 us
    unnamed x1, local copies, waits for them, and re-layouts  1.32 us

profile of v6, /device:TPU:1, one launch (start us, length us, event | category | flops | bytes accessed | tf_op | source)
XLA Modules:
  0.0 63.3 jit_solution(8163223989475341041)
XLA Ops:
  0.0 61.9 %shard_map.73 = f32[8,256,256]{2,1,0:T(8,128)S(1)} custom-call(bf16[2,2,2,8,256,256]{5,4,3,2,1,0:T(8,128)(2,1)} %orb.1, s32[2]{0:T(128)} %kw_in.1, s32[2,2]{1,0:T(2,128)} %occ_in.1, f32[512,512]{1,0:T(8,128)} %zb.1, f32[1,512]{1,0:T(1,128)} %bitcast.1, bf16[4,256,256]{2,1,0:T(8,128)(2,1)} %constant.4.clone.tab_in, f32[8,256]{1,0:T(8,128)} %constant.5.clone.row_in), custom_call_target="tpu_custom_call" | custom-call | tf_op jit(solution)/shard_map/pallas_call | solution.py:323
  62.0 1.3 %copy.9 = f32[8,256,256]{2,1,0:T(8,128)} copy(f32[8,256,256]{2,1,0:T(8,128)S(1)} %shard_map.73) | data formatting | bytes 4194304
